TPU v7x, 32 devices: a whole 2x2x4 slice. The times are simulated.
32 devices in a mesh: ulysses: 8 (over z, x), blk: 4 (over y, core).
Axes of the slice: x: 2, y: 2, z: 4, core: 2. Of those that a mesh axis runs over, the one named last changes fastest.
Arguments:
- queries: bfloat16 [2048, 4096], P(('ulysses', 'blk')), may hold values from -6 to 6
- key_rows: bfloat16 [2048, 1024], P(('ulysses', 'blk')), may hold values from -6 to 6
- value_rows: bfloat16 [2048, 1024], P(('ulysses', 'blk')), may hold values from -6 to 6
Outputs:
- attended: bfloat16 [2048, 4096], P(('ulysses', 'blk'))
All inputs are finite; a program needn't handle non-finite values.
Results may differ from a plain program's by a relative error of at most 0.006.
Values may be sent and summed in bfloat16 or wider, within the bound.
A program may use at most 64 MiB of HBM per device.

v0:
```python
import math

import jax
import jax.numpy as jnp
from jax import lax
from jax.sharding import PartitionSpec as P

Q_HEADS = 32
KV_HEADS = 8
HEAD_DIM = 128


masked_score = -1e30


def from_behind(value, axis, steps):
    count = lax.axis_size(axis)
    pairs = [(source, (source + steps) % count) for source in range(count)]
    return lax.ppermute(value, axis, pairs)


def positions(span_rows, tok_rows, block_count, source):
    index = jnp.arange(span_rows, dtype=jnp.int32)
    return (index // tok_rows * block_count + source) * tok_rows + index % tok_rows


def attend(state, queries_h, block, query_where, key_where, tile_rows):
    span_rows = queries_h.shape[2]
    tile_count = span_rows // tile_rows
    scale = 1.0 / math.sqrt(queries_h.shape[3])

    def per_query(query_tile, carry):
        maxima, totals, sums = carry
        first = query_tile * tile_rows
        q_part = lax.dynamic_slice_in_dim(queries_h, first, tile_rows, 2)
        q_where = lax.dynamic_slice_in_dim(query_where, first, tile_rows, 0)
        inner = (
            lax.dynamic_slice_in_dim(maxima, first, tile_rows, 2),
            lax.dynamic_slice_in_dim(totals, first, tile_rows, 2),
            lax.dynamic_slice_in_dim(sums, first, tile_rows, 2),
        )

        def per_key(key_tile, running):
            top, total, summed = running
            start = key_tile * tile_rows
            kv_part = lax.dynamic_slice_in_dim(block, start, tile_rows, 0)
            k_where = lax.dynamic_slice_in_dim(key_where, start, tile_rows, 0)
            scores = (
                jnp.einsum(
                    "cgtd,scd->cgts",
                    q_part,
                    kv_part[:, :, 0, :],
                    preferred_element_type=jnp.float32,
                )
                * scale
            )
            allowed = k_where[None, :] <= q_where[:, None]
            scores = jnp.where(allowed, scores, masked_score)
            new_top = jnp.maximum(top, jnp.max(scores, axis=-1))
            factor = jnp.exp(top - new_top)
            weights = jnp.where(allowed, jnp.exp(scores - new_top[..., None]), 0.0)
            total = total * factor + jnp.sum(weights, axis=-1)
            summed = summed * factor[..., None] + jnp.einsum(
                "cgts,scd->cgtd",
                weights.astype(jnp.bfloat16),
                kv_part[:, :, 1, :],
                preferred_element_type=jnp.float32,
            )
            return (new_top, total, summed)

        top, total, summed = lax.fori_loop(0, query_tile + 1, per_key, inner)
        maxima = lax.dynamic_update_slice_in_dim(maxima, top, first, 2)
        totals = lax.dynamic_update_slice_in_dim(totals, total, first, 2)
        sums = lax.dynamic_update_slice_in_dim(sums, summed, first, 2)
        return (maxima, totals, sums)

    return lax.fori_loop(0, tile_count, per_query, state)


def per_device(queries, key_rows, value_rows):
    group_size = lax.axis_size("ulysses")
    block_count = lax.axis_size("blk")
    my_block = lax.axis_index("blk")
    tok_rows = queries.shape[0]
    heads_here = Q_HEADS // group_size
    repeat = max(1, group_size // KV_HEADS)
    kv_here = max(1, KV_HEADS // group_size)
    per_kv = heads_here // kv_here
    keys_split = key_rows.reshape(tok_rows, KV_HEADS, 1, HEAD_DIM)
    values_split = value_rows.reshape(tok_rows, KV_HEADS, 1, HEAD_DIM)
    paired = jnp.concatenate((keys_split, values_split), axis=2)
    paired = jnp.broadcast_to(paired[:, :, None], (tok_rows, KV_HEADS, repeat, 2, HEAD_DIM))
    paired = paired.reshape(tok_rows, KV_HEADS * repeat * 2 * HEAD_DIM)
    q_heads, kv_heads = (
        lax.all_to_all(queries, "ulysses", split_axis=1, concat_axis=0, tiled=True),
        lax.all_to_all(paired, "ulysses", split_axis=1, concat_axis=0, tiled=True),
    )
    span_rows = q_heads.shape[0]
    queries_h = q_heads.reshape(span_rows, kv_here, per_kv, HEAD_DIM).transpose(1, 2, 0, 3)
    own_block = kv_heads.reshape(span_rows, kv_here, 2, HEAD_DIM)
    tile_rows = min(512, span_rows)
    query_where = positions(span_rows, tok_rows, block_count, my_block)
    state = (
        jnp.full((kv_here, per_kv, span_rows), masked_score, jnp.float32),
        jnp.zeros((kv_here, per_kv, span_rows), jnp.float32),
        jnp.zeros((kv_here, per_kv, span_rows, HEAD_DIM), jnp.float32),
    )

    def visit(carry, block, source):
        key_where = positions(span_rows, tok_rows, block_count, source)
        return attend(carry, queries_h, block, query_where, key_where, tile_rows)

    state = visit(state, own_block, my_block)
    upward = own_block
    downward = own_block
    for turn in range(1, block_count // 2 + 1):
        upward = from_behind(upward, "blk", 1)
        if turn <= (block_count - 1) // 2:
            downward = from_behind(downward, "blk", -1)
        state = visit(state, upward, (my_block - turn) % block_count)
        if turn <= (block_count - 1) // 2:
            state = visit(state, downward, (my_block + turn) % block_count)
    maxima, totals, sums = state
    mixed = (sums / totals[..., None]).astype(jnp.bfloat16)
    mixed = mixed.transpose(2, 0, 1, 3).reshape(span_rows, heads_here * HEAD_DIM)
    return lax.all_to_all(mixed, "ulysses", split_axis=0, concat_axis=1, tiled=True)


def solution(mesh):
    in_specs = (
        P(("ulysses", "blk"), None),
        P(("ulysses", "blk"), None),
        P(("ulysses", "blk"), None),
    )
    out_specs = P(("ulysses", "blk"), None)
    return jax.shard_map(
        per_device, mesh=mesh, in_specs=in_specs, out_specs=out_specs, check_vma=False
    )
```

profile of v0, /device:TPU:0, one launch (start us, length us, event | category | flops | bytes accessed | tf_op | source)
XLA Modules:
  0.0 70.5 jit_solution(698708769381141740)
XLA Ops:
  0.0 0.9 %copy.53 = bf16[8,8,8,128]{3,2,1,0:T(8,128)(2,1)S(1)} copy(bf16[8,8,8,128]{3,1,2,0:T(8,128)(2,1)} %bitcast.273) | data formatting | bytes 262144
  0.9 0.9 %copy.52 = bf16[8,8,8,128]{3,2,1,0:T(8,128)(2,1)S(1)} copy(bf16[8,8,8,128]{3,1,2,0:T(8,128)(2,1)} %bitcast.274) | data formatting | bytes 262144
  1.9 0.7 %copy.33 = bf16[64,8,256]{2,0,1:T(8,128)(2,1)} copy(bf16[64,8,256]{2,1,0:T(8,128)(2,1)S(1)} %maximum_bitcast_fusion) | data formatting | bytes 524288 | tf_op jit(solution)/shard_map/all_to_all | solution.py:96
  2.7 7.3 %all-to-all-start = ((bf16[64,8,256]{2,0,1:T(8,128)(2,1)}), bf16[64,8,256]{2,0,1:T(8,128)(2,1)S(1)}, u32[]{:S(2)}, u32[]{:S(2)}) async-start(bf16[64,8,256]{2,0,1:T(8,128)(2,1)} %copy.33), calls=%async_computation | async-start | bytes 524288 | tf_op jit(solution)/shard_map/all_to_all | solution.py:96
  9.9 1.9 %copy.79 = bf16[8,8,8,512]{3,2,0,1:T(8,128)(2,1)} copy(bf16[8,8,8,512]{3,2,1,0:T(8,128)(2,1)} %bitcast.270) | data formatting | bytes 1048576 | tf_op jit(solution)/shard_map/all_to_all | solution.py:95
  11.8 7.0 %all-to-all-done = bf16[64,8,256]{2,0,1:T(8,128)(2,1)S(1)} async-done(((bf16[64,8,256]{2,0,1:T(8,128)(2,1)}), bf16[64,8,256]{2,0,1:T(8,128)(2,1)S(1)}, u32[]{:S(2)}, u32[]{:S(2)}) %all-to-all-start) | async-done | bytes 262176 | tf_op jit(solution)/shard_map/all_to_all | solution.py:96
  18.9 3.6 %all-to-all-start.1 = ((bf16[64,8,512]{2,0,1:T(8,128)(2,1)}), bf16[64,8,512]{2,0,1:T(8,128)(2,1)S(1)}, u32[]{:S(2)}, u32[]{:S(2)}) async-start(bf16[64,8,512]{2,0,1:T(8,128)(2,1)} %bitcast.266), calls=%async_computation.1 | async-start | bytes 1048576 | tf_op jit(solution)/shard_map/all_to_all | solution.py:95
  22.7 0.7 %broadcast_compare_fusion.3 = (pred[512,512]{0,1:T(8,128)(4,1)S(1)}, pred[512,512]{0,1:T(8,128)(4,1)S(1)}, pred[512,512]{0,1:T(8,128)(4,1)S(1)}, pred[512,512]{0,1:T(8,128)(4,1)S(1)}) fusion(s32[512]{0:T(512)S(1)} %multiply_add_fusion.3, s32[512]{0:T(512)S(1)} %multiply_add_fusion.1, s32[512]{0:T(512)S(1)} %multiply_add_fusion, s32[512]{0:T(512)S(1)} %multiply_add_fusion.2), kind=kLoop, calls=%fused_computation.53 | loop fusion | flops 1048576 | bytes 1056768 | tf_op jit(solution)/shard_map/while/body/eval_jaxpr/while/body/le | solution.py:57
  23.4 1.8 %collective-permute-start.1 = (bf16[512,1,2,128]{3,0,2,1:T(8,128)(2,1)S(1)}, bf16[512,1,2,128]{3,0,2,1:T(8,128)(2,1)S(1)}, u32[]{:S(2)}, u32[]{:S(2)}) collective-permute-start(bf16[512,1,2,128]{3,0,2,1:T(8,128)(2,1)S(1)} %copy.34), channel_id=1, source_target_pairs={{0,3},{1,0},{2,1},{3,2},{4,7},{5,4},{6,5},{7,6},{8,11},{9,8},{10,9... | collective-permute-start | bytes 786440 | tf_op jit(solution)/shard_map/ppermute | solution.py:19
  25.2 3.5 %collective-permute-done = bf16[512,1,2,128]{3,0,2,1:T(8,128)(2,1)S(1)} collective-permute-done((bf16[512,1,2,128]{3,0,2,1:T(8,128)(2,1)S(1)}, bf16[512,1,2,128]{3,0,2,1:T(8,128)(2,1)S(1)}, u32[]{:S(2)}, u32[]{:S(2)}) %collective-permute-start) | collective-permute-done | bytes 262176 | tf_op jit(solution)/shard_map/ppermute | solution.py:19
  28.8 7.8 %all-to-all-done.1 = bf16[64,8,512]{2,0,1:T(8,128)(2,1)S(1)} async-done(((bf16[64,8,512]{2,0,1:T(8,128)(2,1)}), bf16[64,8,512]{2,0,1:T(8,128)(2,1)S(1)}, u32[]{:S(2)}, u32[]{:S(2)}) %all-to-all-start.1) | async-done | bytes 524320 | tf_op jit(solution)/shard_map/all_to_all | solution.py:95
  36.7 0.9 %fusion = (f32[4,512]{1,0:T(4,128)S(1)}, f32[512,4,512]{2,0,1:T(8,128)S(1)}) fusion(pred[512,512]{0,1:T(8,128)(4,1)S(1)} %get-tuple-element.340, bf16[512,1,4,128]{3,2,0,1:T(4,128)(2,1)S(1)} %reshape.228, bf16[512,1,2,128]{3,0,2,1:T(8,128)(2,1)S(1)} %copy.34), kind=kOutput, calls=%fused_computation.8 | convolution fusion | flops 271579136 | bytes 5120000 | tf_op jit(solution)/shard_map/while/body/eval_jaxpr/while/body/cgtd,scd->cgts/dot_general | solution.py:49
  37.7 1.0 %fusion.4 = f32[4,512]{1,0:T(4,128)S(1)} fusion(f32[512,4,512]{2,0,1:T(8,128)S(1)} %get-tuple-element.351, f32[4,512]{1,0:T(4,128)S(1)} %broadcast_maximum_fusion, pred[512,512]{0,1:T(8,128)(4,1)S(1)} %get-tuple-element.340), kind=kLoop, calls=%fused_computation.12 | loop fusion | flops 5240832 | bytes 4472832 | tf_op jit(solution)/shard_map/while/body/eval_jaxpr/while/body/reduce_sum | solution.py:62
  38.7 0.9 %fusion.1 = (f32[4,512]{1,0:T(4,128)S(1)}, f32[512,4,512]{2,0,1:T(8,128)S(1)}) fusion(pred[512,512]{0,1:T(8,128)(4,1)S(1)} %get-tuple-element.343, bf16[512,1,4,128]{3,2,0,1:T(4,128)(2,1)S(1)} %reshape.228, bf16[512,1,2,128]{3,0,2,1:T(8,128)(2,1)S(1)} %collective-permute-done), kind=kOutput, calls=%fused_computation.9 | convolution fusion | flops 271579136 | bytes 5120000 | tf_op jit(solution)/shard_map/while/body/eval_jaxpr/while/body/cgtd,scd->cgts/dot_general | solution.py:49
  39.6 0.9 %fusion.2 = (f32[4,512]{1,0:T(4,128)S(1)}, f32[512,4,512]{2,0,1:T(8,128)S(1)}) fusion(pred[512,512]{0,1:T(8,128)(4,1)S(1)} %get-tuple-element.341, bf16[512,1,4,128]{3,2,0,1:T(4,128)(2,1)S(1)} %reshape.228, bf16[512,1,2,128]{3,0,2,1:T(8,128)(2,1)S(1)} %collective-permute-done.1), kind=kOutput, calls=%fused_computation.10 | convolution fusion | flops 271579136 | bytes 5120000 | tf_op jit(solution)/shard_map/while/body/eval_jaxpr/while/body/cgtd,scd->cgts/dot_general | solution.py:49
  40.5 0.9 %fusion.3 = (f32[4,512]{1,0:T(4,128)S(1)}, f32[512,4,512]{2,0,1:T(8,128)S(1)}) fusion(pred[512,512]{0,1:T(8,128)(4,1)S(1)} %get-tuple-element.342, bf16[512,1,4,128]{3,2,0,1:T(4,128)(2,1)S(1)} %reshape.228, bf16[512,1,2,128]{3,0,2,1:T(8,128)(2,1)S(1)} %collective-permute-done.2), kind=kOutput, calls=%fused_computation.11 | convolution fusion | flops 271579136 | bytes 5120000 | tf_op jit(solution)/shard_map/while/body/eval_jaxpr/while/body/cgtd,scd->cgts/dot_general | solution.py:49
  41.5 1.1 %fusion.10 = f32[4,512]{1,0:T(4,128)S(1)} fusion(f32[512,4,512]{2,0,1:T(8,128)S(1)} %get-tuple-element.345, f32[4,512]{1,0:T(4,128)S(1)} %get-tuple-element.333, pred[512,512]{0,1:T(8,128)(4,1)S(1)} %get-tuple-element.342), kind=kLoop, calls=%fused_computation.18 | loop fusion | flops 5240832 | bytes 4472832 | tf_op jit(solution)/shard_map/while/body/eval_jaxpr/while/body/reduce_sum | solution.py:62
  42.5 2.3 %fusion.6 = (f32[4,512]{1,0:T(4,128)S(1)}, f32[4,512]{1,0:T(4,128)S(1)}) fusion(f32[512,4,512]{2,0,1:T(8,128)S(1)} %get-tuple-element.349, f32[4,512]{1,0:T(4,128)S(1)} %bitcast.275, pred[512,512]{0,1:T(8,128)(4,1)S(1)} %get-tuple-element.343, f32[4,512]{1,0:T(4,128)S(1)} %fusion.106, f32[512,4,512]{2,0,1:T(8,128)S(1)} %get-tuple-element.347, ...), kind=kLoop, calls=%fused_computation.14 | loop fusion | flops 10481664 | bytes 8945664 | tf_op jit(solution)/shard_map/while/body/eval_jaxpr/while/body/reduce_sum | solution.py:62
  44.8 1.6 %fusion.54 = f32[1,4,512,128]{3,2,1,0:T(8,128)S(1)} fusion(f32[512,4,512]{2,0,1:T(8,128)S(1)} %get-tuple-element.351, f32[4,512]{1,0:T(4,128)S(1)} %broadcast_maximum_fusion, pred[512,512]{0,1:T(8,128)(4,1)S(1)} %get-tuple-element.340, f32[4,512]{1,0:T(4,128)S(1)} %get-tuple-element.338, f32[4,512]{1,0:T(4,128)S(1)} %get-tuple-element.339, ...), kind=kOutput, calls=%fused_computation.38 | convolution fusion | flops 274202624 | bytes 5660672 | tf_op jit(solution)/shard_map/while/body/eval_jaxpr/while/body/cgts,scd->cgtd/dot_general | solution.py:63
  46.5 1.4 %fusion.30 = f32[1,4,512,128]{3,2,1,0:T(8,128)S(1)} fusion(f32[512,4,512]{2,0,1:T(8,128)S(1)} %get-tuple-element.347, f32[4,512]{1,0:T(4,128)S(1)} %fusion.106, pred[512,512]{0,1:T(8,128)(4,1)S(1)} %get-tuple-element.341, bf16[512,1,2,128]{3,0,2,1:T(8,128)(2,1)S(1)} %collective-permute-done.1), kind=kOutput, calls=%fused_computation.30 | convolution fusion | flops 273678336 | bytes 5644288 | tf_op jit(solution)/shard_map/while/body/eval_jaxpr/while/body/cgts,scd->cgtd/dot_general | solution.py:63
  47.8 1.6 %fusion.48 = f32[1,4,512,128]{3,2,1,0:T(8,128)S(1)} fusion(f32[1,4,512,128]{3,2,1,0:T(8,128)S(1)} %fusion.30, f32[1,4,512,128]{3,2,1,0:T(8,128)S(1)} %fusion.54, f32[512,4,512]{2,0,1:T(8,128)S(1)} %get-tuple-element.349, f32[4,512]{1,0:T(4,128)S(1)} %bitcast.276, pred[512,512]{0,1:T(8,128)(4,1)S(1)} %get-tuple-element.343, ...), kind=kOutput, calls=%fused_computation.36 | convolution fusion | flops 274726912 | bytes 7757824 | tf_op jit(solution)/shard_map/while/body/eval_jaxpr/while/body/cgts,scd->cgtd/dot_general | solution.py:63
  49.5 1.7 %fusion.59 = bf16[512,1,4,128]{3,0,2,1:T(8,128)(2,1)S(1)} fusion(f32[1,4,512,128]{3,2,1,0:T(8,128)S(1)} %fusion.48, f32[512,4,512]{2,0,1:T(8,128)S(1)} %get-tuple-element.345, f32[4,512]{1,0:T(4,128)S(1)} %get-tuple-element.333, pred[512,512]{0,1:T(8,128)(4,1)S(1)} %get-tuple-element.342, f32[4,512]{1,0:T(4,128)S(1)} %get-tuple-element.335, ...), kind=kOutput, calls=%fused_computation.40 | convolution fusion | flops 274464768 | bytes 6176768 | tf_op jit(solution)/shard_map/while/body/eval_jaxpr/while/body/cgts,scd->cgtd/dot_general | solution.py:63
  51.8 17.9 %all_to_all.51 = bf16[8,64,512]{2,1,0:T(8,128)(2,1)S(1)} all-to-all(bf16[8,64,512]{2,1,0:T(8,128)(2,1)S(1)} %all_to_all.44), channel_id=1, replica_groups=mesh['ulysses'=8,'blk'=4] {'ulysses'}, dimensions={0} | all-to-all | bytes 1048576 | tf_op jit(solution)/shard_map/all_to_all | solution.py:126
  69.7 0.8 %copy.51 = bf16[8,8,8,512]{3,2,0,1:T(8,128)(2,1)} copy(bf16[8,8,8,512]{3,2,1,0:T(8,128)(2,1)S(1)} %bitcast.268) | data formatting | bytes 1048576 | tf_op jit(solution)/shard_map/all_to_all | solution.py:126
  (18 shorter events, 1.2 us)
Async XLA Ops:
  2.7 16.2 %all-to-all-start = ((bf16[64,8,256]{2,0,1:T(8,128)(2,1)}), bf16[64,8,256]{2,0,1:T(8,128)(2,1)S(1)}, u32[]{:S(2)}, u32[]{:S(2)}) async-start(bf16[64,8,256]{2,0,1:T(8,128)(2,1)} %copy.33), calls=%async_computation | async-start | bytes 524288 | tf_op jit(solution)/shard_map/all_to_all | solution.py:96
  18.9 17.8 %all-to-all-start.1 = ((bf16[64,8,512]{2,0,1:T(8,128)(2,1)}), bf16[64,8,512]{2,0,1:T(8,128)(2,1)S(1)}, u32[]{:S(2)}, u32[]{:S(2)}) async-start(bf16[64,8,512]{2,0,1:T(8,128)(2,1)} %bitcast.266), calls=%async_computation.1 | async-start | bytes 1048576 | tf_op jit(solution)/shard_map/all_to_all | solution.py:95
  22.6 6.1 %collective-permute-start = (bf16[512,1,2,128]{3,0,2,1:T(8,128)(2,1)S(1)}, bf16[512,1,2,128]{3,0,2,1:T(8,128)(2,1)S(1)}, u32[]{:S(2)}, u32[]{:S(2)}) collective-permute-start(bf16[512,1,2,128]{3,0,2,1:T(8,128)(2,1)S(1)} %copy.34), channel_id=1, source_target_pairs={{0,1},{1,2},{2,3},{3,0},{4,5},{5,6},{6,7},{7,4},{8,9},{9,10},{10,1... | collective-permute-start | bytes 786440 | tf_op jit(solution)/shard_map/ppermute | solution.py:19
  23.4 16.2 %collective-permute-start.1 = (bf16[512,1,2,128]{3,0,2,1:T(8,128)(2,1)S(1)}, bf16[512,1,2,128]{3,0,2,1:T(8,128)(2,1)S(1)}, u32[]{:S(2)}, u32[]{:S(2)}) collective-permute-start(bf16[512,1,2,128]{3,0,2,1:T(8,128)(2,1)S(1)} %copy.34), channel_id=1, source_target_pairs={{0,3},{1,0},{2,1},{3,2},{4,7},{5,4},{6,5},{7,6},{8,11},{9,8},{10,9... | collective-permute-start | bytes 786440 | tf_op jit(solution)/shard_map/ppermute | solution.py:19
  28.7 11.8 %collective-permute-start.2 = (bf16[512,1,2,128]{3,0,2,1:T(8,128)(2,1)S(1)}, bf16[512,1,2,128]{3,0,2,1:T(8,128)(2,1)S(1)}, u32[]{:S(2)}, u32[]{:S(2)}) collective-permute-start(bf16[512,1,2,128]{3,0,2,1:T(8,128)(2,1)S(1)} %collective-permute-done), channel_id=1, source_target_pairs={{0,1},{1,2},{2,3},{3,0},{4,5},{5,6},{6,7},{7,4},{8,9},{9,10},{10,1... | collective-permute-start | bytes 786440 | tf_op jit(solution)/shard_map/ppermute | solution.py:19
where the time goes:
time: 70.9 us; the launch traced here: 70.5 us
  waiting for transfers between devices  18.3 us (26%)
  blocking collectives  17.9 us (25%)
  starting transfers between devices  12.8 us (18%)
  matrix products  9.87 us (14%)
  local copies, waits for them, and re-layouts  6.14 us (9%)
  other arithmetic  5.26 us (7%)
    all_to_all x1, blocking collectives, per_device(): lax.all_to_all(mixed, 'ulysses', split_axis=0, concat_axis=1, tiled=True)  17.9 us
    all_to_all x1, waiting for transfers between devices, per_device(): lax.all_to_all(queries, 'ulysses', split_axis=1, concat_axis=0, tiled=True)  7.78 us
    all_to_all x1, starting transfers between devices, per_device(): lax.all_to_all(paired, 'ulysses', split_axis=1, concat_axis=0, tiled=True)  7.28 us
    all_to_all x1, waiting for transfers between devices, per_device(): lax.all_to_all(paired, 'ulysses', split_axis=1, concat_axis=0, tiled=True)  7.04 us
    dot_general x4, matrix products, per_key(): jnp.einsum('cgts,scd->cgtd', weights.astype(jnp.bfloat16), kv_part[:, :,...  6.3 us
    reduce_sum x3, other arithmetic, per_key(): total = total * factor + jnp.sum(weights, axis=-1)  4.4 us
    all_to_all x1, starting transfers between devices, per_device(): lax.all_to_all(queries, 'ulysses', split_axis=1, concat_axis=0, tiled=True)  3.59 us
    dot_general x4, matrix products, per_key(): jnp.einsum('cgtd,scd->cgts', q_part, kv_part[:, :, 0, :], preferred_eleme...  3.57 us
  transfers between devices with their start and end apart: 5, of which 3 were waited for; matrix products, arithmetic and copies ran while one was open for 9% of the time, Pallas kernels for 0%

commit v1 on v0

v1 whole, which is shorter than its diff:
```python
import functools
import math

import jax
import jax.numpy as jnp
from jax import lax
from jax.experimental import pallas as pl
from jax.experimental.pallas import tpu as pltpu
from jax.sharding import PartitionSpec as P

Q_HEADS = 32
KV_HEADS = 8
HEAD_DIM = 128
GROUP = Q_HEADS // KV_HEADS
MESH = pl.DeviceIdType.MESH
masked_score = -1e30


def kernel(
    ulysses, blk, q_ref, k_ref, v_ref, out_ref,
    qbuf, kbuf, vbuf, obuf, top, total, summed,
    local_sem, kv_send, kv_recv, q_send, q_recv, up_send, relay_send, up_recv, o_send, o_recv,
):
    members = KV_HEADS
    across = members // blk
    slabs = ulysses // across
    tok = q_ref.shape[0]
    rows = members * tok
    half_rows = rows // 2
    width = GROUP * HEAD_DIM
    factor = math.log2(math.e) / math.sqrt(HEAD_DIM)
    cores = 2 if blk % 2 == 0 else 1

    u = lax.axis_index("ulysses")
    b = lax.axis_index("blk")
    slab = u // across
    mx = u % across
    mine = mx * blk + b

    peers = []
    for dx in range(across):
        for dy in range(blk // cores):
            for dc in range(cores):
                px = (mx + dx) % across
                pb = (b // cores + dy) % (blk // cores) * cores + (b % cores + dc) % cores
                peers.append((px * blk + pb, (slab * across + px, pb)))
    above = (u + across, b)
    below = (u - across, b)

    barrier = pltpu.get_barrier_semaphore()
    for _, device in peers[1:]:
        pl.semaphore_signal(barrier, inc=1, device_id=device, device_id_type=MESH)

    @pl.when(slab < slabs - 1)
    def _():
        pl.semaphore_signal(barrier, inc=1, device_id=above, device_id_type=MESH)

    @pl.when(slab > 0)
    def _():
        pl.semaphore_signal(barrier, inc=1, device_id=below, device_id_type=MESH)

    neighbours = jnp.minimum(slab, 1) + jnp.minimum(slabs - 1 - slab, 1)
    pl.semaphore_wait(barrier, members - 1 + neighbours)

    def at(start, size):
        return pl.ds(pl.multiple_of(start, tok), size)

    def cols(head, size):
        return pl.ds(pl.multiple_of(head * size, size), size)

    own_rows = at(slab * rows + mine * tok, tok)
    stores = ((k_ref, kbuf), (v_ref, vbuf))

    kv_copies = []
    for i, (peer, device) in enumerate(peers):
        if i == 0:
            continue
        for which, (source, store) in enumerate(stores):
            copy = pltpu.make_async_remote_copy(
                src_ref=source.at[:, cols(peer, HEAD_DIM)],
                dst_ref=store.at[own_rows],
                send_sem=kv_send.at[i, which],
                recv_sem=kv_recv.at[mine, which],
                device_id=device,
                device_id_type=MESH,
            )
            copy.start()
            kv_copies.append(copy)
    local_copies = []
    for which, (source, store) in enumerate(stores):
        copy = pltpu.make_async_copy(
            source.at[:, cols(mine, HEAD_DIM)], store.at[own_rows], local_sem.at[which]
        )
        copy.start()
        local_copies.append(copy)
    q_copies = []
    for i, (peer, device) in enumerate(peers):
        if i == 0:
            continue
        copy = pltpu.make_async_remote_copy(
            src_ref=q_ref.at[:, cols(peer, width)],
            dst_ref=qbuf.at[at(mine * tok, tok)],
            send_sem=q_send.at[i],
            recv_sem=q_recv.at[mine],
            device_id=device,
            device_id_type=MESH,
        )
        copy.start()
        q_copies.append(copy)
    q_local = pltpu.make_async_copy(
        q_ref.at[:, cols(mine, width)], qbuf.at[at(mine * tok, tok)], local_sem.at[2]
    )
    q_local.start()

    def wait_bytes(ref, sem):
        pltpu.make_async_copy(ref, ref, sem).wait()

    def upward(i):
        peer = peers[i][0]
        where = at(slab * rows + peer * tok, tok)
        half = peer // (members // 2)
        return [
            pltpu.make_async_remote_copy(
                src_ref=store.at[where],
                dst_ref=store.at[where],
                send_sem=up_send.at[i, which],
                recv_sem=up_recv.at[slab, half, which],
                device_id=above,
                device_id_type=MESH,
            )
            for which, (_, store) in enumerate(stores)
        ]

    for i, (peer, _) in enumerate(peers):
        where = at(slab * rows + peer * tok, tok)
        for which, (_, store) in enumerate(stores):
            if i == 0:
                local_copies[which].wait()
            else:
                wait_bytes(store.at[where], kv_recv.at[peer, which])

        @pl.when(slab < slabs - 1)
        def _():
            for copy in upward(i):
                copy.start()

    def chunk_of(t):
        source = slab - 1 - t // 2
        half = (mine // (members // 2) + t % 2) % 2
        return source, half, at(source * rows + half * half_rows, half_rows)

    def relay(t):
        source, half, where = chunk_of(t)
        return [
            pltpu.make_async_remote_copy(
                src_ref=store.at[where],
                dst_ref=store.at[where],
                send_sem=relay_send.at[source, half, which],
                recv_sem=up_recv.at[source, half, which],
                device_id=above,
                device_id_type=MESH,
            )
            for which, (_, store) in enumerate(stores)
        ]

    def take(t):
        source, half, where = chunk_of(t)
        for which, (_, store) in enumerate(stores):
            wait_bytes(store.at[where], up_recv.at[source, half, which])

        @pl.when(slab < slabs - 1)
        def _():
            for copy in relay(t):
                copy.start()

    @pl.when(slab > 0)
    def _():
        take(0)
        take(1)

    q_local.wait()
    for peer, _ in peers[1:]:
        wait_bytes(qbuf.at[at(peer * tok, tok)], q_recv.at[peer])

    def block(head, q_rows, key_rows, masked, first):
        q = qbuf[q_rows, head * HEAD_DIM : (head + 1) * HEAD_DIM]
        scores = lax.dot_general(
            q, kbuf[key_rows, :], (((1,), (1,)), ((), ())), preferred_element_type=jnp.float32
        ) * factor
        if masked:
            down = lax.broadcasted_iota(jnp.int32, scores.shape, 0)
            right = lax.broadcasted_iota(jnp.int32, scores.shape, 1)
            scores = jnp.where(right <= down, scores, masked_score)
        peak = jnp.max(scores, axis=1, keepdims=True)
        size = scores.shape[0]
        if first:
            new_top = jnp.broadcast_to(peak, (size, HEAD_DIM))
        else:
            old_top = top[head, q_rows]
            new_top = jnp.maximum(old_top, peak)
        repeats = scores.shape[1] // HEAD_DIM
        weights = jnp.exp2(scores - jnp.concatenate([new_top] * repeats, axis=1))
        if masked:
            weights = jnp.where(right <= down, weights, 0.0)
        part = weights[:, :HEAD_DIM]
        for r in range(1, repeats):
            part = part + weights[:, r * HEAD_DIM : (r + 1) * HEAD_DIM]
        mixed = jnp.dot(
            weights.astype(jnp.bfloat16), vbuf[key_rows, :], preferred_element_type=jnp.float32
        )
        if first:
            total[head, q_rows] = part
            summed[head, q_rows] = mixed
        else:
            shrink = jnp.exp2(old_top - new_top)
            total[head, q_rows] = total[head, q_rows] * shrink + part
            summed[head, q_rows] = summed[head, q_rows] * shrink + mixed
        top[head, q_rows] = new_top

    low, high = pl.ds(0, half_rows), pl.ds(half_rows, half_rows)
    own_low = at(slab * rows, half_rows)
    own_high = at(slab * rows + half_rows, half_rows)
    for head in range(GROUP):
        block(head, low, own_low, True, True)
        block(head, high, own_low, False, True)
        block(head, high, own_high, True, False)

    def visit(t, carry):
        @pl.when(t >= 2)
        def _():
            take(t)

        where = chunk_of(t)[2]
        for head in range(GROUP):
            for q_rows in (low, high):
                block(head, q_rows, where, False, False)
        return carry

    lax.fori_loop(0, 2 * slab, visit, 0)

    def finish(peer):
        where = at(peer * tok, tok)
        for head in range(GROUP):
            sums = jnp.sum(total[head, where], axis=1, keepdims=True)
            obuf[where, head * HEAD_DIM : (head + 1) * HEAD_DIM] = (
                summed[head, where] / sums
            ).astype(jnp.bfloat16)

    o_copies = []
    for i in reversed(range(1, members)):
        peer, device = peers[i]
        finish(peer)
        copy = pltpu.make_async_remote_copy(
            src_ref=obuf.at[at(peer * tok, tok)],
            dst_ref=out_ref.at[:, cols(mine, width)],
            send_sem=o_send.at[i],
            recv_sem=o_recv.at[mine],
            device_id=device,
            device_id_type=MESH,
        )
        copy.start()
        o_copies.append(copy)
    finish(mine)
    o_local = pltpu.make_async_copy(
        obuf.at[at(mine * tok, tok)], out_ref.at[:, cols(mine, width)], local_sem.at[3]
    )
    o_local.start()

    for copy in kv_copies + q_copies:
        copy.wait_send()

    @pl.when(slab < slabs - 1)
    def _():
        for i in range(members):
            for copy in upward(i):
                copy.wait_send()

        def sent(t, carry):
            for copy in relay(t):
                copy.wait_send()
            return carry

        lax.fori_loop(0, 2 * slab, sent, 0)

    for copy in o_copies:
        copy.wait_send()
    o_local.wait()
    for peer, _ in peers[1:]:
        wait_bytes(out_ref.at[:, cols(peer, width)], o_recv.at[peer])


def solution(mesh):
    ulysses, blk = mesh.shape["ulysses"], mesh.shape["blk"]
    members = KV_HEADS
    assert members % blk == 0 and ulysses % (members // blk) == 0
    slabs = ulysses // (members // blk)

    def per_device(queries, key_rows, value_rows):
        tok = queries.shape[0]
        rows = members * tok
        seq = slabs * rows
        dma = pltpu.SemaphoreType.DMA
        return pl.pallas_call(
            functools.partial(kernel, ulysses, blk),
            out_shape=jax.ShapeDtypeStruct(queries.shape, queries.dtype),
            in_specs=[pl.BlockSpec(memory_space=pltpu.VMEM)] * 3,
            out_specs=pl.BlockSpec(memory_space=pltpu.VMEM),
            scratch_shapes=[
                pltpu.VMEM((rows, GROUP * HEAD_DIM), jnp.bfloat16),
                pltpu.VMEM((seq, HEAD_DIM), jnp.bfloat16),
                pltpu.VMEM((seq, HEAD_DIM), jnp.bfloat16),
                pltpu.VMEM((rows, GROUP * HEAD_DIM), jnp.bfloat16),
                pltpu.VMEM((GROUP, rows, HEAD_DIM), jnp.float32),
                pltpu.VMEM((GROUP, rows, HEAD_DIM), jnp.float32),
                pltpu.VMEM((GROUP, rows, HEAD_DIM), jnp.float32),
                dma((4,)),
                dma((members, 2)),
                dma((members, 2)),
                dma((members,)),
                dma((members,)),
                dma((members, 2)),
                dma((slabs, 2, 2)),
                dma((slabs, 2, 2)),
                dma((members,)),
                dma((members,)),
            ],
            compiler_params=pltpu.CompilerParams(collective_id=0, has_side_effects=True),
        )(queries, key_rows, value_rows)

    spec = P(("ulysses", "blk"), None)
    return jax.shard_map(
        per_device, mesh=mesh, in_specs=(spec, spec, spec), out_specs=spec, check_vma=False
    )
```

time: 70.9 us -> 37.8 us (0.53)
  the two profiles are of different devices: /device:TPU:0 before, /device:TPU:24 now
where the time goes in v1:
time: 37.8 us; the launch traced here: 37.6 us
  Pallas kernels  35.8 us (95%)
  local copies, waits for them, and re-layouts  1.87 us (5%)
    pallas_call x1, Pallas kernels, per_device(): pl.pallas_call(functools.partial(kernel, ulysses, blk), out_shape=jax.Sha...  35.8 us
    unnamed x1, local copies, waits for them, and re-layouts  1.87 us

profile of v1, /device:TPU:24, one launch (start us, length us, event | category | flops | bytes accessed | tf_op | source)
XLA Modules:
  0.0 37.6 jit_solution(13282137862392948191)
XLA Ops:
  0.0 35.8 %shard_map.37 = bf16[64,4096]{1,0:T(8,128)(2,1)} custom-call(bf16[64,4096]{1,0:T(8,128)(2,1)} %q_ref.1, bf16[64,1024]{1,0:T(8,128)(2,1)} %k_ref.1, bf16[64,1024]{1,0:T(8,128)(2,1)} %v_ref.1), custom_call_target="tpu_custom_call" | custom-call | tf_op jit(solution)/shard_map/pallas_call | solution.py:303
  35.8 1.9 %copy.5 = bf16[64,4096]{1,0:T(8,128)(2,1)} copy(bf16[64,4096]{1,0:T(8,128)(2,1)} %shard_map.37) | data formatting | bytes 1048576

commit v2 on v1

--- a/solution.py
+++ b/solution.py
@@ -17,14 +17,21 @@
 
 
 def kernel(
-    ulysses, blk, q_ref, k_ref, v_ref, out_ref,
+    ulysses, blk, q_hbm, k_hbm, v_hbm, out_ref,
+    q_ref, k_ref, v_ref,
     qbuf, kbuf, vbuf, obuf, top, total, summed,
-    local_sem, kv_send, kv_recv, q_send, q_recv, up_send, relay_send, up_recv, o_send, o_recv,
+    local_sem, kv_send, kv_recv, q_send, q_recv, up_send, relay_send, up_recv, o_send, o_recv, go_sem,
 ):
     members = KV_HEADS
     across = members // blk
     slabs = ulysses // across
     tok = q_ref.shape[0]
+    loads = [
+        pltpu.make_async_copy(source, store, local_sem.at[4 + i])
+        for i, (source, store) in enumerate(((k_hbm, k_ref), (v_hbm, v_ref), (q_hbm, q_ref)))
+    ]
+    for load in loads:
+        load.start()
     rows = members * tok
     half_rows = rows // 2
     width = GROUP * HEAD_DIM
@@ -41,9 +48,13 @@
     for dx in range(across):
         for dy in range(blk // cores):
             for dc in range(cores):
+                core = (b % cores + dc) % cores if dx == dy == 0 else dc
                 px = (mx + dx) % across
-                pb = (b // cores + dy) % (blk // cores) * cores + (b % cores + dc) % cores
+                pb = (b // cores + dy) % (blk // cores) * cores + core
                 peers.append((px * blk + pb, (slab * across + px, pb)))
+    lead = b % cores == 0
+    partner = peers[cores - 1][1]
+    turns = list(range(1, cores)) + [i for c in range(cores) for i in range(cores + c, members, cores)]
     above = (u + across, b)
     below = (u - across, b)
 
@@ -72,9 +83,10 @@
     stores = ((k_ref, kbuf), (v_ref, vbuf))
 
     kv_copies = []
-    for i, (peer, device) in enumerate(peers):
-        if i == 0:
-            continue
+    for load in loads[:2]:
+        load.wait()
+    for i in turns:
+        peer, device = peers[i]
         for which, (source, store) in enumerate(stores):
             copy = pltpu.make_async_remote_copy(
                 src_ref=source.at[:, cols(peer, HEAD_DIM)],
@@ -94,9 +106,9 @@
         copy.start()
         local_copies.append(copy)
     q_copies = []
-    for i, (peer, device) in enumerate(peers):
-        if i == 0:
-            continue
+    loads[2].wait()
+    for i in turns:
+        peer, device = peers[i]
         copy = pltpu.make_async_remote_copy(
             src_ref=q_ref.at[:, cols(peer, width)],
             dst_ref=qbuf.at[at(mine * tok, tok)],
@@ -139,7 +151,7 @@
             else:
                 wait_bytes(store.at[where], kv_recv.at[peer, which])
 
-        @pl.when(slab < slabs - 1)
+        @pl.when((slab < slabs - 1) & lead)
         def _():
             for copy in upward(i):
                 copy.start()
@@ -173,10 +185,33 @@
             for copy in relay(t):
                 copy.start()
 
-    @pl.when(slab > 0)
+    ahead = 4
+
+    def pass_on():
+        if cores > 1:
+            @pl.when(slab < slabs - 1)
+            def _():
+                pl.semaphore_signal(go_sem, inc=1, device_id=partner, device_id_type=MESH)
+
+    def take_one(t, carry):
+        take(t)
+        return carry
+
+    @pl.when(lead)
     def _():
-        take(0)
-        take(1)
+        lax.fori_loop(0, jnp.minimum(ahead, 2 * slab), take_one, 0)
+
+        @pl.when(2 * slab <= ahead)
+        def _():
+            pass_on()
+
+    if cores > 1:
+        @pl.when((slab < slabs - 1) & (b % cores != 0))
+        def _():
+            pl.semaphore_wait(go_sem, 1)
+            for i in range(members):
+                for copy in upward(i):
+                    copy.start()
 
     q_local.wait()
     for peer, _ in peers[1:]:
@@ -226,9 +261,13 @@
         block(head, high, own_high, True, False)
 
     def visit(t, carry):
-        @pl.when(t >= 2)
+        @pl.when((t >= ahead) | (b % cores != 0))
         def _():
             take(t)
+
+        @pl.when((t >= ahead) & (t == 2 * slab - 1) & lead)
+        def _():
+            pass_on()
 
         where = chunk_of(t)[2]
         for head in range(GROUP):
@@ -303,9 +342,12 @@
         return pl.pallas_call(
             functools.partial(kernel, ulysses, blk),
             out_shape=jax.ShapeDtypeStruct(queries.shape, queries.dtype),
-            in_specs=[pl.BlockSpec(memory_space=pltpu.VMEM)] * 3,
-            out_specs=pl.BlockSpec(memory_space=pltpu.VMEM),
+            in_specs=[pl.BlockSpec(memory_space=pl.ANY)] * 3,
+            out_specs=pl.BlockSpec(memory_space=pl.ANY),
             scratch_shapes=[
+                pltpu.VMEM(queries.shape, queries.dtype),
+                pltpu.VMEM(key_rows.shape, key_rows.dtype),
+                pltpu.VMEM(value_rows.shape, value_rows.dtype),
                 pltpu.VMEM((rows, GROUP * HEAD_DIM), jnp.bfloat16),
                 pltpu.VMEM((seq, HEAD_DIM), jnp.bfloat16),
                 pltpu.VMEM((seq, HEAD_DIM), jnp.bfloat16),
@@ -313,7 +355,7 @@
                 pltpu.VMEM((GROUP, rows, HEAD_DIM), jnp.float32),
                 pltpu.VMEM((GROUP, rows, HEAD_DIM), jnp.float32),
                 pltpu.VMEM((GROUP, rows, HEAD_DIM), jnp.float32),
-                dma((4,)),
+                dma((7,)),
                 dma((members, 2)),
                 dma((members, 2)),
                 dma((members,)),
@@ -323,6 +365,7 @@
                 dma((slabs, 2, 2)),
                 dma((members,)),
                 dma((members,)),
+                pltpu.SemaphoreType.REGULAR,
             ],
             compiler_params=pltpu.CompilerParams(collective_id=0, has_side_effects=True),
         )(queries, key_rows, value_rows)

time: 37.8 us -> 37 us (0.979)
  Pallas kernels: 35.8 us -> 34.9 us
    pallas_call x1, Pallas kernels: 35.8 us -> 34.9 us  [per_device(): pl.pallas_call(functools.partial(kernel, ulysses, blk), out_shape=jax.Sha...]
where the time goes in v2:
time: 37 us; the launch traced here: 36.8 us
  Pallas kernels  34.9 us (94%)
  local copies, waits for them, and re-layouts  1.87 us (5%)
    pallas_call x1, Pallas kernels, per_device(): pl.pallas_call(functools.partial(kernel, ulysses, blk), out_shape=jax.Sha...  34.9 us
    unnamed x1, local copies, waits for them, and re-layouts  1.87 us

profile of v2, /device:TPU:24, one launch (start us, length us, event | category | flops | bytes accessed | tf_op | source)
XLA Modules:
  0.0 36.8 jit_solution(2877896083121296849)
XLA Ops:
  0.0 34.9 %shard_map.37 = bf16[64,4096]{1,0:T(8,128)(2,1)} custom-call(bf16[64,4096]{1,0:T(8,128)(2,1)} %q_hbm.1, bf16[64,1024]{1,0:T(8,128)(2,1)} %k_hbm.1, bf16[64,1024]{1,0:T(8,128)(2,1)} %v_hbm.1), custom_call_target="tpu_custom_call" | custom-call | tf_op jit(solution)/shard_map/pallas_call | solution.py:342
  34.9 1.9 %copy.5 = bf16[64,4096]{1,0:T(8,128)(2,1)} copy(bf16[64,4096]{1,0:T(8,128)(2,1)} %shard_map.37) | data formatting | bytes 1048576

commit v3 on v2

--- a/solution.py
+++ b/solution.py
@@ -151,7 +151,7 @@
             else:
                 wait_bytes(store.at[where], kv_recv.at[peer, which])
 
-        @pl.when((slab < slabs - 1) & lead)
+        @pl.when(slab < slabs - 1)
         def _():
             for copy in upward(i):
                 copy.start()
@@ -185,33 +185,21 @@
             for copy in relay(t):
                 copy.start()
 
-    ahead = 4
-
-    def pass_on():
-        if cores > 1:
-            @pl.when(slab < slabs - 1)
-            def _():
-                pl.semaphore_signal(go_sem, inc=1, device_id=partner, device_id_type=MESH)
-
-    def take_one(t, carry):
-        take(t)
-        return carry
-
-    @pl.when(lead)
+    relaying = (slab > 0) & (slab < slabs - 1)
+    if cores > 1:
+        @pl.when(relaying & (b % cores != 0))
+        def _():
+            pl.semaphore_wait(go_sem, 1)
+
+    @pl.when(slab > 0)
     def _():
-        lax.fori_loop(0, jnp.minimum(ahead, 2 * slab), take_one, 0)
-
-        @pl.when(2 * slab <= ahead)
-        def _():
-            pass_on()
+        take(0)
+        take(1)
 
     if cores > 1:
-        @pl.when((slab < slabs - 1) & (b % cores != 0))
-        def _():
-            pl.semaphore_wait(go_sem, 1)
-            for i in range(members):
-                for copy in upward(i):
-                    copy.start()
+        @pl.when(relaying & lead)
+        def _():
+            pl.semaphore_signal(go_sem, inc=1, device_id=partner, device_id_type=MESH)
 
     q_local.wait()
     for peer, _ in peers[1:]:
@@ -261,13 +249,9 @@
         block(head, high, own_high, True, False)
 
     def visit(t, carry):
-        @pl.when((t >= ahead) | (b % cores != 0))
+        @pl.when(t >= 2)
         def _():
             take(t)
-
-        @pl.when((t >= ahead) & (t == 2 * slab - 1) & lead)
-        def _():
-            pass_on()
 
         where = chunk_of(t)[2]
         for head in range(GROUP):

time: 37 us -> 35.3 us (0.954)
  Pallas kernels: 34.9 us -> 33.2 us
    pallas_call x1, Pallas kernels: 34.9 us -> 33.2 us  [per_device(): pl.pallas_call(functools.partial(kernel, ulysses, blk), out_shape=jax.Sha...]
where the time goes in v3:
time: 35.3 us; the launch traced here: 35.1 us
  Pallas kernels  33.2 us (94%)
  local copies, waits for them, and re-layouts  1.87 us (5%)
    pallas_call x1, Pallas kernels, per_device(): pl.pallas_call(functools.partial(kernel, ulysses, blk), out_shape=jax.Sha...  33.2 us
    unnamed x1, local copies, waits for them, and re-layouts  1.87 us

profile of v3, /device:TPU:24, one launch (start us, length us, event | category | flops | bytes accessed | tf_op | source)
XLA Modules:
  0.0 35.1 jit_solution(4923282336731157098)
XLA Ops:
  0.0 33.2 %shard_map.37 = bf16[64,4096]{1,0:T(8,128)(2,1)} custom-call(bf16[64,4096]{1,0:T(8,128)(2,1)} %q_hbm.1, bf16[64,1024]{1,0:T(8,128)(2,1)} %k_hbm.1, bf16[64,1024]{1,0:T(8,128)(2,1)} %v_hbm.1), custom_call_target="tpu_custom_call" | custom-call | tf_op jit(solution)/shard_map/pallas_call | solution.py:326
  33.2 1.9 %copy.5 = bf16[64,4096]{1,0:T(8,128)(2,1)} copy(bf16[64,4096]{1,0:T(8,128)(2,1)} %shard_map.37) | data formatting | bytes 1048576

commit v4 on v3

--- a/solution.py
+++ b/solution.py
@@ -259,7 +259,19 @@
                 block(head, q_rows, where, False, False)
         return carry
 
-    lax.fori_loop(0, 2 * slab, visit, 0)
+    lax.fori_loop(0, 2 * slab - 1, visit, 0)
+    last = 2 * slab - 1
+
+    @pl.when(slab > 1)
+    def _():
+        take(last)
+
+    def last_block(part):
+        @pl.when(slab > 0)
+        def _():
+            where = chunk_of(last)[2]
+            for head in range(GROUP):
+                block(head, at(part * half_rows, half_rows), where, False, False)
 
     def finish(peer):
         where = at(peer * tok, tok)
@@ -269,8 +281,13 @@
                 summed[head, where] / sums
             ).astype(jnp.bfloat16)
 
+    own_part = mine // (members // 2)
+    last_block(1 - own_part)
+    split = members // 2 if across == 2 else 1
     o_copies = []
     for i in reversed(range(1, members)):
+        if i == split - 1 or (split == 1 and i == members - 1):
+            last_block(own_part)
         peer, device = peers[i]
         finish(peer)
         copy = pltpu.make_async_remote_copy(

time: 35.3 us -> 34.9 us (0.989)
  no operation moved by 1% of the time
where the time goes in v4:
time: 34.9 us; the launch traced here: 34.7 us
  Pallas kernels  32.9 us (94%)
  local copies, waits for them, and re-layouts  1.87 us (5%)
    pallas_call x1, Pallas kernels, per_device(): pl.pallas_call(functools.partial(kernel, ulysses, blk), out_shape=jax.Sha...  32.9 us
    unnamed x1, local copies, waits for them, and re-layouts  1.87 us

profile of v4, /device:TPU:24, one launch (start us, length us, event | category | flops | bytes accessed | tf_op | source)
XLA Modules:
  0.0 34.7 jit_solution(8323182374163230391)
XLA Ops:
  0.0 32.9 %shard_map.37 = bf16[64,4096]{1,0:T(8,128)(2,1)} custom-call(bf16[64,4096]{1,0:T(8,128)(2,1)} %q_hbm.1, bf16[64,1024]{1,0:T(8,128)(2,1)} %k_hbm.1, bf16[64,1024]{1,0:T(8,128)(2,1)} %v_hbm.1), custom_call_target="tpu_custom_call" | custom-call | tf_op jit(solution)/shard_map/pallas_call | solution.py:343
  32.9 1.9 %copy.5 = bf16[64,4096]{1,0:T(8,128)(2,1)} copy(bf16[64,4096]{1,0:T(8,128)(2,1)} %shard_map.37) | data formatting | bytes 1048576
